TPU v7x, 32 devices: a whole 2x2x4 slice. The times are simulated.
32 devices in a mesh: section: 8 (over y, x, core), dp: 4 (over z).
Axes of the slice: x: 2, y: 2, z: 4, core: 2. Of those that a mesh axis runs over, the one named last changes fastest.
Arguments:
- out_pair: float32 [512, 2048], P('dp'), may hold values from -6 to 6
- out_grad: bfloat16 [512, 2048], P('dp'), may hold values from -6 to 6
- f_weight: bfloat16 [8, 1024, 1024], P('section', 'dp'), may hold values from -0.09375 to 0.09375
- g_weight: bfloat16 [8, 1024, 1024], P('section', 'dp'), may hold values from -0.09375 to 0.09375
- gains: float32 [8, 2, 1024], P('section'), may hold values from 0.1 to 1.9
Outputs:
- in_pair: float32 [8, 512, 2048], P('section', 'dp')
- in_grad: bfloat16 [8, 512, 2048], P('section', 'dp')
- f_grad: float32 [8, 1024, 1024], P('section', 'dp')
- g_grad: float32 [8, 1024, 1024], P('section', 'dp')
- gains_grad: float32 [8, 2, 1024], P('section')
All inputs are finite; a program needn't handle non-finite values.
Results may differ from a plain program's by a relative error of at most 0.04.
Values may be sent and summed in bfloat16 or wider, within the bound.
A program may use at most 64 MiB of HBM per device.

v0:
```python
import jax
import jax.numpy as jnp
from jax import lax
from jax.sharding import PartitionSpec as P

offset = 0.25


def from_behind(array, axis, by):
    devices = lax.axis_size(axis)
    pairs = [(i, i + by) for i in range(devices) if 0 <= i + by < devices]
    return lax.ppermute(array, axis, pairs)


def silu_parts(pre_values):
    sigmoid_value = jax.nn.sigmoid(pre_values)
    return (pre_values * sigmoid_value, sigmoid_value * (1.0 + pre_values * (1.0 - sigmoid_value)))


def normalize(values, gain_row):
    inv_scale = lax.rsqrt(jnp.mean(values * values, axis=-1, keepdims=True) + offset)
    return ((values * inv_scale * gain_row).astype(jnp.bfloat16), inv_scale)


def norm_back(values, inv_scale, gain_row, upstream):
    weighted = gain_row * upstream
    cubed = inv_scale * inv_scale * inv_scale
    return inv_scale * weighted - values * cubed * jnp.mean(
        weighted * values, axis=-1, keepdims=True
    )


def times_transposed(delta, weight_full):
    return lax.dot_general(
        delta, weight_full, (((1,), (1,)), ((), ())), preferred_element_type=jnp.float32
    )


def coupling_back(upper_out, lower_out, upper_grad, lower_grad, w_first, w_second, gain_pair):
    normed_second, scale_second = normalize(upper_out, gain_pair[1])
    pre_second = jnp.dot(normed_second, w_second, preferred_element_type=jnp.float32)
    act_second, slope_second = silu_parts(pre_second)
    lower_in = lower_out - act_second
    normed_first, scale_first = normalize(lower_in, gain_pair[0])
    pre_first = jnp.dot(normed_first, w_first, preferred_element_type=jnp.float32)
    act_first, slope_first = silu_parts(pre_first)
    upper_in = upper_out - act_first
    delta_second = (lower_grad * slope_second).astype(jnp.bfloat16)
    back_second = times_transposed(delta_second, w_second)
    through = upper_grad + norm_back(upper_out, scale_second, gain_pair[1], back_second)
    delta_first = (through * slope_first).astype(jnp.bfloat16)
    back_first = times_transposed(delta_first, w_first)
    lower_total = lower_grad + norm_back(lower_in, scale_first, gain_pair[0], back_first)
    gain_terms = jnp.stack(
        [
            jnp.sum(back_first * lower_in * scale_first, axis=0),
            jnp.sum(back_second * upper_out * scale_second, axis=0),
        ]
    )
    return (
        upper_in,
        lower_in,
        through.astype(jnp.bfloat16),
        lower_total.astype(jnp.bfloat16),
        normed_first,
        delta_first,
        normed_second,
        delta_second,
        gain_terms,
    )


def shards(out_pair, out_grad, f_weight, g_weight, gains):
    sections = lax.axis_size("section")
    section_index = lax.axis_index("section")
    w_first, w_second = (
        lax.all_gather(f_weight[0], "dp", axis=0, tiled=True),
        lax.all_gather(g_weight[0], "dp", axis=0, tiled=True),
    )
    gain_pair = gains[0]
    row_count = out_pair.shape[0]
    pair_width = out_pair.shape[1]
    channels = pair_width // 2
    blocks = 4
    block_rows = row_count // blocks
    tick_count = blocks + sections - 1
    is_last = section_index == sections - 1

    def tick(tick_index, loop_state):
        pair_in, grad_in = (loop_state[0], loop_state[1])
        buffers = loop_state[2:]
        block_index = tick_index - (sections - 1 - section_index)
        active = jnp.logical_and(block_index >= 0, block_index < blocks)
        row_start = jnp.clip(block_index, 0, blocks - 1) * block_rows
        pair_here = jnp.where(
            is_last, lax.dynamic_slice_in_dim(out_pair, row_start, block_rows, 0), pair_in
        )
        grad_here = jnp.where(
            is_last, lax.dynamic_slice_in_dim(out_grad, row_start, block_rows, 0), grad_in
        )

        def compute(held):
            pair_buf, grad_buf, first_norms, first_deltas, second_norms, second_deltas, gain_acc = (
                held
            )
            results = coupling_back(
                pair_here[:, :channels],
                pair_here[:, channels:],
                grad_here[:, :channels].astype(jnp.float32),
                grad_here[:, channels:].astype(jnp.float32),
                w_first,
                w_second,
                gain_pair,
            )
            new_pair = jnp.concatenate([results[0], results[1]], axis=1)
            new_grad = jnp.concatenate([results[2], results[3]], axis=1)
            return (
                lax.dynamic_update_slice_in_dim(pair_buf, new_pair, row_start, 0),
                lax.dynamic_update_slice_in_dim(grad_buf, new_grad, row_start, 0),
                lax.dynamic_update_slice_in_dim(first_norms, results[4], row_start, 0),
                lax.dynamic_update_slice_in_dim(first_deltas, results[5], row_start, 0),
                lax.dynamic_update_slice_in_dim(second_norms, results[6], row_start, 0),
                lax.dynamic_update_slice_in_dim(second_deltas, results[7], row_start, 0),
                gain_acc + results[8],
                new_pair,
                new_grad,
            )

        def unchanged(held):
            return held + (
                jnp.zeros((block_rows, pair_width), jnp.float32),
                jnp.zeros((block_rows, pair_width), jnp.bfloat16),
            )

        updated = lax.cond(active, compute, unchanged, buffers)
        sent_pair = from_behind(updated[7].astype(jnp.bfloat16), "section", -1).astype(jnp.float32)
        sent_grad = from_behind(updated[8], "section", -1)
        return (sent_pair, sent_grad) + updated[:7]

    initial = (
        jnp.zeros((block_rows, pair_width), jnp.float32),
        jnp.zeros((block_rows, pair_width), jnp.bfloat16),
        jnp.zeros((row_count, pair_width), jnp.float32),
        jnp.zeros((row_count, pair_width), jnp.bfloat16),
        jnp.zeros((row_count, channels), jnp.bfloat16),
        jnp.zeros((row_count, channels), jnp.bfloat16),
        jnp.zeros((row_count, channels), jnp.bfloat16),
        jnp.zeros((row_count, channels), jnp.bfloat16),
        jnp.zeros((2, channels), jnp.float32),
    )
    final_state = lax.fori_loop(0, tick_count, tick, initial)
    pair_buf, grad_buf, first_norms, first_deltas, second_norms, second_deltas, gain_acc = (
        final_state[2:]
    )
    contract_rows = (((0,), (0,)), ((), ()))
    first_part = lax.dot_general(
        first_norms, first_deltas, contract_rows, preferred_element_type=jnp.float32
    )
    second_part = lax.dot_general(
        second_norms, second_deltas, contract_rows, preferred_element_type=jnp.float32
    )
    first_sum, second_sum = (
        lax.psum_scatter(
            first_part.astype(jnp.bfloat16), "dp", scatter_dimension=0, tiled=True
        ).astype(jnp.float32),
        lax.psum_scatter(
            second_part.astype(jnp.bfloat16), "dp", scatter_dimension=0, tiled=True
        ).astype(jnp.float32),
    )
    gain_total = lax.psum(gain_acc, "dp")
    return (pair_buf[None], grad_buf[None], first_sum[None], second_sum[None], gain_total[None])


def solution(mesh):
    placed = (
        P("dp", None),
        P("dp", None),
        P("section", "dp", None),
        P("section", "dp", None),
        P("section", None, None),
    )
    return jax.shard_map(
        shards,
        mesh=mesh,
        in_specs=placed,
        out_specs=(
            P("section", "dp", None),
            P("section", "dp", None),
            P("section", "dp", None),
            P("section", "dp", None),
            P("section", None, None),
        ),
        check_vma=False,
    )
```

profile of v0, /device:TPU:0, one launch (start us, length us, event | category | flops | bytes accessed | tf_op | source)
XLA Modules:
  0.0 364.0 jit_solution(3674701004738925881)
XLA Ops:
  8.7 49.2 %all-gather.5.cloned.1.call-done = bf16[1,1024,1024]{2,1,0:T(8,128)(2,1)} async-done(((bf16[1,256,1024]{2,1,0:T(8,128)(2,1)}), bf16[1,1024,1024]{2,1,0:T(8,128)(2,1)}) %all-gather.5.cloned.1.call-update) | async-done | bytes 2097168 | tf_op jit(solution)/shard_map/all_gather | solution.py:78
  58.0 46.1 %all-gather.7.cloned.1.call-done = bf16[1,1024,1024]{2,1,0:T(8,128)(2,1)} async-done(((bf16[1,256,1024]{2,1,0:T(8,128)(2,1)}), bf16[1,1024,1024]{2,1,0:T(8,128)(2,1)}) %all-gather.7.cloned.1.call-update) | async-done | bytes 2097168 | tf_op jit(solution)/shard_map/all_gather | solution.py:77
  106.8 156.3 %while.32 = (s32[]{:T(128)}, f32[32,2048]{1,0:T(8,128)S(1)}, bf16[32,2048]{1,0:T(8,128)(2,1)S(1)}, f32[128,2048]{1,0:T(8,128)}, bf16[128,2048]{1,0:T(8,128)(2,1)...) while((s32[]{:T(128)}, f32[32,2048]{1,0:T(8,128)S(1)}, ...), condition=%wide.region_9.10_spmd.clone, body=%wide.region_0.9_spmd.clone.sunk | while | flops 271812800 | bytes 24069820 | solution.py:151
  114.8 3.7 %collective-permute-done = bf16[32,2048]{1,0:T(8,128)(2,1)S(1)} collective-permute-done((bf16[32,2048]{1,0:T(8,128)(2,1)S(1)}, bf16[32,2048]{1,0:T(8,128)(2,1)S(1)}, u32[]{:S(2)}, u32[]{:S(2)}) %collective-permute-start) | collective-permute-done | bytes 131104 | tf_op jit(solution)/shard_map/while/body/eval_jaxpr/ppermute | solution.py:12
  123.0 3.7 %collective-permute-done = bf16[32,2048]{1,0:T(8,128)(2,1)S(1)} collective-permute-done((bf16[32,2048]{1,0:T(8,128)(2,1)S(1)}, bf16[32,2048]{1,0:T(8,128)(2,1)S(1)}, u32[]{:S(2)}, u32[]{:S(2)}) %collective-permute-start) | collective-permute-done | bytes 131104 | tf_op jit(solution)/shard_map/while/body/eval_jaxpr/ppermute | solution.py:12
  131.3 3.7 %collective-permute-done = bf16[32,2048]{1,0:T(8,128)(2,1)S(1)} collective-permute-done((bf16[32,2048]{1,0:T(8,128)(2,1)S(1)}, bf16[32,2048]{1,0:T(8,128)(2,1)S(1)}, u32[]{:S(2)}, u32[]{:S(2)}) %collective-permute-start) | collective-permute-done | bytes 131104 | tf_op jit(solution)/shard_map/while/body/eval_jaxpr/ppermute | solution.py:12
  135.0 1.9 collective-permute-done.1
  139.6 3.7 %collective-permute-done = bf16[32,2048]{1,0:T(8,128)(2,1)S(1)} collective-permute-done((bf16[32,2048]{1,0:T(8,128)(2,1)S(1)}, bf16[32,2048]{1,0:T(8,128)(2,1)S(1)}, u32[]{:S(2)}, u32[]{:S(2)}) %collective-permute-start) | collective-permute-done | bytes 131104 | tf_op jit(solution)/shard_map/while/body/eval_jaxpr/ppermute | solution.py:12
  147.8 3.7 %collective-permute-done = bf16[32,2048]{1,0:T(8,128)(2,1)S(1)} collective-permute-done((bf16[32,2048]{1,0:T(8,128)(2,1)S(1)}, bf16[32,2048]{1,0:T(8,128)(2,1)S(1)}, u32[]{:S(2)}, u32[]{:S(2)}) %collective-permute-start) | collective-permute-done | bytes 131104 | tf_op jit(solution)/shard_map/while/body/eval_jaxpr/ppermute | solution.py:12
  156.1 42.6 %collective-permute-done = bf16[32,2048]{1,0:T(8,128)(2,1)S(1)} collective-permute-done((bf16[32,2048]{1,0:T(8,128)(2,1)S(1)}, bf16[32,2048]{1,0:T(8,128)(2,1)S(1)}, u32[]{:S(2)}, u32[]{:S(2)}) %collective-permute-start) | collective-permute-done | bytes 131104 | tf_op jit(solution)/shard_map/while/body/eval_jaxpr/ppermute | solution.py:12
  200.6 7.5 %conditional.3 = (f32[128,2048]{1,0:T(8,128)}, bf16[128,2048]{1,0:T(8,128)(2,1)}, bf16[128,1024]{1,0:T(8,128)(2,1)S(1)}, bf16[128,1024]{1,0:T(8,128)(2,1)S(1)}, ...) conditional(s32[]{:T(128)} %convert_element_type.140, ...), branch_computations={%region_1.1_spmd, %region_2.8_spmd.clone} | conditional | flops 271747264 | bytes 22627530 | solution.py:135
  210.7 4.6 %collective-permute-done = bf16[32,2048]{1,0:T(8,128)(2,1)S(1)} collective-permute-done((bf16[32,2048]{1,0:T(8,128)(2,1)S(1)}, bf16[32,2048]{1,0:T(8,128)(2,1)S(1)}, u32[]{:S(2)}, u32[]{:S(2)}) %collective-permute-start) | collective-permute-done | bytes 131104 | tf_op jit(solution)/shard_map/while/body/eval_jaxpr/ppermute | solution.py:12
  217.2 7.5 %conditional.3 = (f32[128,2048]{1,0:T(8,128)}, bf16[128,2048]{1,0:T(8,128)(2,1)}, bf16[128,1024]{1,0:T(8,128)(2,1)S(1)}, bf16[128,1024]{1,0:T(8,128)(2,1)S(1)}, ...) conditional(s32[]{:T(128)} %convert_element_type.140, ...), branch_computations={%region_1.1_spmd, %region_2.8_spmd.clone} | conditional | flops 271747264 | bytes 22627530 | solution.py:135
  227.3 4.6 %collective-permute-done = bf16[32,2048]{1,0:T(8,128)(2,1)S(1)} collective-permute-done((bf16[32,2048]{1,0:T(8,128)(2,1)S(1)}, bf16[32,2048]{1,0:T(8,128)(2,1)S(1)}, u32[]{:S(2)}, u32[]{:S(2)}) %collective-permute-start) | collective-permute-done | bytes 131104 | tf_op jit(solution)/shard_map/while/body/eval_jaxpr/ppermute | solution.py:12
  233.8 7.5 %conditional.3 = (f32[128,2048]{1,0:T(8,128)}, bf16[128,2048]{1,0:T(8,128)(2,1)}, bf16[128,1024]{1,0:T(8,128)(2,1)S(1)}, bf16[128,1024]{1,0:T(8,128)(2,1)S(1)}, ...) conditional(s32[]{:T(128)} %convert_element_type.140, ...), branch_computations={%region_1.1_spmd, %region_2.8_spmd.clone} | conditional | flops 271747264 | bytes 22627530 | solution.py:135
  243.9 4.6 %collective-permute-done = bf16[32,2048]{1,0:T(8,128)(2,1)S(1)} collective-permute-done((bf16[32,2048]{1,0:T(8,128)(2,1)S(1)}, bf16[32,2048]{1,0:T(8,128)(2,1)S(1)}, u32[]{:S(2)}, u32[]{:S(2)}) %collective-permute-start) | collective-permute-done | bytes 131104 | tf_op jit(solution)/shard_map/while/body/eval_jaxpr/ppermute | solution.py:12
  250.4 7.5 %conditional.3 = (f32[128,2048]{1,0:T(8,128)}, bf16[128,2048]{1,0:T(8,128)(2,1)}, bf16[128,1024]{1,0:T(8,128)(2,1)S(1)}, bf16[128,1024]{1,0:T(8,128)(2,1)S(1)}, ...) conditional(s32[]{:T(128)} %convert_element_type.140, ...), branch_computations={%region_1.1_spmd, %region_2.8_spmd.clone} | conditional | flops 271747264 | bytes 22627530 | solution.py:135
  263.1 3.0 convolution_convert_fusion
  266.2 2.1 convolution_convert_fusion.1
  268.2 10.8 %psum.7 = f32[1,2,1024]{2,1,0:T(2,128)} all-reduce(f32[1,2,1024]{2,1,0:T(2,128)S(1)} %bitcast.42), channel_id=1, replica_groups=mesh['section'=8,'dp'=4] {'dp'}, use_global_device_ids=true, to_apply=%region_12.13 | all-reduce | flops 2048 | bytes 16384 | tf_op jit(solution)/shard_map/psum | solution.py:170
  279.0 31.6 %reduce-scatter.5.cloned.1.call-done = bf16[256,1024]{1,0:T(8,128)(2,1)} async-done(((bf16[1024,1024]{1,0:T(8,128)(2,1)}), bf16[256,1024]{1,0:T(8,128)(2,1)}) %reduce-scatter.5.cloned.1.call-update) | async-done | bytes 524304 | tf_op jit(solution)/shard_map/reduce_scatter | solution.py:166
  310.6 2.1 bitcast_convert_fusion
  312.7 42.6 %reduce-scatter.3.cloned.1.call-done = bf16[256,1024]{1,0:T(8,128)(2,1)} async-done(((bf16[1024,1024]{1,0:T(8,128)(2,1)}), bf16[256,1024]{1,0:T(8,128)(2,1)}) %reduce-scatter.3.cloned.1.call-update) | async-done | bytes 524304 | tf_op jit(solution)/shard_map/reduce_scatter | solution.py:163
  355.3 2.1 bitcast_convert_fusion.1
  (163 shorter events, 83.6 us)
Async XLA Ops:
  7.2 50.8 %all-gather.5.cloned.1.call-start = ((), (), s32[]{:S(2)}) async-start(), calls=%async_computation.4 | async-start | bytes 2621440 | tf_op jit(solution)/shard_map/all_gather | solution.py:78
  7.9 96.1 %all-gather.7.cloned.1.call-start = ((), (), s32[]{:S(2)}) async-start(), calls=%async_computation.5 | async-start | bytes 2621440 | tf_op jit(solution)/shard_map/all_gather | solution.py:77
  8.7 302.0 %reduce-scatter.5.cloned.1.call-start = ((), (), s32[]{:S(2)}) async-start(), calls=%async_computation.3 | async-start | bytes 2621440 | tf_op jit(solution)/shard_map/reduce_scatter | solution.py:166
  108.2 3.9 %collective-permute-start.1 = (bf16[32,2048]{1,0:T(8,128)(2,1)S(1)}, bf16[32,2048]{1,0:T(8,128)(2,1)S(1)}, u32[]{:S(2)}, u32[]{:S(2)}) collective-permute-start(bf16[32,2048]{1,0:T(8,128)(2,1)S(1)} %get-tuple-element.961), channel_id=1, source_target_pairs={{4,0},{8,4},{12,8},{16,12},{20,16},{24,20},{28,24},{5,1},{9,5},{13... | collective-permute-start | bytes 393224 | tf_op jit(solution)/shard_map/while/body/eval_jaxpr/ppermute | solution.py:12
  112.2 6.3 %collective-permute-start = (bf16[32,2048]{1,0:T(8,128)(2,1)S(1)}, bf16[32,2048]{1,0:T(8,128)(2,1)S(1)}, u32[]{:S(2)}, u32[]{:S(2)}) collective-permute-start(bf16[32,2048]{1,0:T(8,128)(2,1)S(1)} %get-tuple-element.960), channel_id=1, source_target_pairs={{4,0},{8,4},{12,8},{16,12},{20,16},{24,20},{28,24},{5,1},{9,5},{13... | collective-permute-start | bytes 393224 | tf_op jit(solution)/shard_map/while/body/eval_jaxpr/ppermute | solution.py:12
  113.5 6.9 %collective-permute-start.1 = (bf16[32,2048]{1,0:T(8,128)(2,1)S(1)}, bf16[32,2048]{1,0:T(8,128)(2,1)S(1)}, u32[]{:S(2)}, u32[]{:S(2)}) collective-permute-start(bf16[32,2048]{1,0:T(8,128)(2,1)S(1)} %get-tuple-element.961), channel_id=1, source_target_pairs={{4,0},{8,4},{12,8},{16,12},{20,16},{24,20},{28,24},{5,1},{9,5},{13... | collective-permute-start | bytes 393224 | tf_op jit(solution)/shard_map/while/body/eval_jaxpr/ppermute | solution.py:12
  120.4 6.3 %collective-permute-start = (bf16[32,2048]{1,0:T(8,128)(2,1)S(1)}, bf16[32,2048]{1,0:T(8,128)(2,1)S(1)}, u32[]{:S(2)}, u32[]{:S(2)}) collective-permute-start(bf16[32,2048]{1,0:T(8,128)(2,1)S(1)} %get-tuple-element.960), channel_id=1, source_target_pairs={{4,0},{8,4},{12,8},{16,12},{20,16},{24,20},{28,24},{5,1},{9,5},{13... | collective-permute-start | bytes 393224 | tf_op jit(solution)/shard_map/while/body/eval_jaxpr/ppermute | solution.py:12
  121.7 6.9 %collective-permute-start.1 = (bf16[32,2048]{1,0:T(8,128)(2,1)S(1)}, bf16[32,2048]{1,0:T(8,128)(2,1)S(1)}, u32[]{:S(2)}, u32[]{:S(2)}) collective-permute-start(bf16[32,2048]{1,0:T(8,128)(2,1)S(1)} %get-tuple-element.961), channel_id=1, source_target_pairs={{4,0},{8,4},{12,8},{16,12},{20,16},{24,20},{28,24},{5,1},{9,5},{13... | collective-permute-start | bytes 393224 | tf_op jit(solution)/shard_map/while/body/eval_jaxpr/ppermute | solution.py:12
  128.7 6.3 %collective-permute-start = (bf16[32,2048]{1,0:T(8,128)(2,1)S(1)}, bf16[32,2048]{1,0:T(8,128)(2,1)S(1)}, u32[]{:S(2)}, u32[]{:S(2)}) collective-permute-start(bf16[32,2048]{1,0:T(8,128)(2,1)S(1)} %get-tuple-element.960), channel_id=1, source_target_pairs={{4,0},{8,4},{12,8},{16,12},{20,16},{24,20},{28,24},{5,1},{9,5},{13... | collective-permute-start | bytes 393224 | tf_op jit(solution)/shard_map/while/body/eval_jaxpr/ppermute | solution.py:12
  130.0 6.9 %collective-permute-start.1 = (bf16[32,2048]{1,0:T(8,128)(2,1)S(1)}, bf16[32,2048]{1,0:T(8,128)(2,1)S(1)}, u32[]{:S(2)}, u32[]{:S(2)}) collective-permute-start(bf16[32,2048]{1,0:T(8,128)(2,1)S(1)} %get-tuple-element.961), channel_id=1, source_target_pairs={{4,0},{8,4},{12,8},{16,12},{20,16},{24,20},{28,24},{5,1},{9,5},{13... | collective-permute-start | bytes 393224 | tf_op jit(solution)/shard_map/while/body/eval_jaxpr/ppermute | solution.py:12
  137.0 6.3 %collective-permute-start = (bf16[32,2048]{1,0:T(8,128)(2,1)S(1)}, bf16[32,2048]{1,0:T(8,128)(2,1)S(1)}, u32[]{:S(2)}, u32[]{:S(2)}) collective-permute-start(bf16[32,2048]{1,0:T(8,128)(2,1)S(1)} %get-tuple-element.960), channel_id=1, source_target_pairs={{4,0},{8,4},{12,8},{16,12},{20,16},{24,20},{28,24},{5,1},{9,5},{13... | collective-permute-start | bytes 393224 | tf_op jit(solution)/shard_map/while/body/eval_jaxpr/ppermute | solution.py:12
  138.3 6.9 %collective-permute-start.1 = (bf16[32,2048]{1,0:T(8,128)(2,1)S(1)}, bf16[32,2048]{1,0:T(8,128)(2,1)S(1)}, u32[]{:S(2)}, u32[]{:S(2)}) collective-permute-start(bf16[32,2048]{1,0:T(8,128)(2,1)S(1)} %get-tuple-element.961), channel_id=1, source_target_pairs={{4,0},{8,4},{12,8},{16,12},{20,16},{24,20},{28,24},{5,1},{9,5},{13... | collective-permute-start | bytes 393224 | tf_op jit(solution)/shard_map/while/body/eval_jaxpr/ppermute | solution.py:12
  145.2 6.3 %collective-permute-start = (bf16[32,2048]{1,0:T(8,128)(2,1)S(1)}, bf16[32,2048]{1,0:T(8,128)(2,1)S(1)}, u32[]{:S(2)}, u32[]{:S(2)}) collective-permute-start(bf16[32,2048]{1,0:T(8,128)(2,1)S(1)} %get-tuple-element.960), channel_id=1, source_target_pairs={{4,0},{8,4},{12,8},{16,12},{20,16},{24,20},{28,24},{5,1},{9,5},{13... | collective-permute-start | bytes 393224 | tf_op jit(solution)/shard_map/while/body/eval_jaxpr/ppermute | solution.py:12
  146.5 6.9 %collective-permute-start.1 = (bf16[32,2048]{1,0:T(8,128)(2,1)S(1)}, bf16[32,2048]{1,0:T(8,128)(2,1)S(1)}, u32[]{:S(2)}, u32[]{:S(2)}) collective-permute-start(bf16[32,2048]{1,0:T(8,128)(2,1)S(1)} %get-tuple-element.961), channel_id=1, source_target_pairs={{4,0},{8,4},{12,8},{16,12},{20,16},{24,20},{28,24},{5,1},{9,5},{13... | collective-permute-start | bytes 393224 | tf_op jit(solution)/shard_map/while/body/eval_jaxpr/ppermute | solution.py:12
  153.5 45.2 %collective-permute-start = (bf16[32,2048]{1,0:T(8,128)(2,1)S(1)}, bf16[32,2048]{1,0:T(8,128)(2,1)S(1)}, u32[]{:S(2)}, u32[]{:S(2)}) collective-permute-start(bf16[32,2048]{1,0:T(8,128)(2,1)S(1)} %get-tuple-element.960), channel_id=1, source_target_pairs={{4,0},{8,4},{12,8},{16,12},{20,16},{24,20},{28,24},{5,1},{9,5},{13... | collective-permute-start | bytes 393224 | tf_op jit(solution)/shard_map/while/body/eval_jaxpr/ppermute | solution.py:12
  154.8 45.8 %collective-permute-start.1 = (bf16[32,2048]{1,0:T(8,128)(2,1)S(1)}, bf16[32,2048]{1,0:T(8,128)(2,1)S(1)}, u32[]{:S(2)}, u32[]{:S(2)}) collective-permute-start(bf16[32,2048]{1,0:T(8,128)(2,1)S(1)} %get-tuple-element.961), channel_id=1, source_target_pairs={{4,0},{8,4},{12,8},{16,12},{20,16},{24,20},{28,24},{5,1},{9,5},{13... | collective-permute-start | bytes 393224 | tf_op jit(solution)/shard_map/while/body/eval_jaxpr/ppermute | solution.py:12
  208.1 7.2 %collective-permute-start = (bf16[32,2048]{1,0:T(8,128)(2,1)S(1)}, bf16[32,2048]{1,0:T(8,128)(2,1)S(1)}, u32[]{:S(2)}, u32[]{:S(2)}) collective-permute-start(bf16[32,2048]{1,0:T(8,128)(2,1)S(1)} %get-tuple-element.960), channel_id=1, source_target_pairs={{4,0},{8,4},{12,8},{16,12},{20,16},{24,20},{28,24},{5,1},{9,5},{13... | collective-permute-start | bytes 393224 | tf_op jit(solution)/shard_map/while/body/eval_jaxpr/ppermute | solution.py:12
  209.4 7.8 %collective-permute-start.1 = (bf16[32,2048]{1,0:T(8,128)(2,1)S(1)}, bf16[32,2048]{1,0:T(8,128)(2,1)S(1)}, u32[]{:S(2)}, u32[]{:S(2)}) collective-permute-start(bf16[32,2048]{1,0:T(8,128)(2,1)S(1)} %get-tuple-element.961), channel_id=1, source_target_pairs={{4,0},{8,4},{12,8},{16,12},{20,16},{24,20},{28,24},{5,1},{9,5},{13... | collective-permute-start | bytes 393224 | tf_op jit(solution)/shard_map/while/body/eval_jaxpr/ppermute | solution.py:12
  224.7 7.2 %collective-permute-start = (bf16[32,2048]{1,0:T(8,128)(2,1)S(1)}, bf16[32,2048]{1,0:T(8,128)(2,1)S(1)}, u32[]{:S(2)}, u32[]{:S(2)}) collective-permute-start(bf16[32,2048]{1,0:T(8,128)(2,1)S(1)} %get-tuple-element.960), channel_id=1, source_target_pairs={{4,0},{8,4},{12,8},{16,12},{20,16},{24,20},{28,24},{5,1},{9,5},{13... | collective-permute-start | bytes 393224 | tf_op jit(solution)/shard_map/while/body/eval_jaxpr/ppermute | solution.py:12
  226.0 7.8 %collective-permute-start.1 = (bf16[32,2048]{1,0:T(8,128)(2,1)S(1)}, bf16[32,2048]{1,0:T(8,128)(2,1)S(1)}, u32[]{:S(2)}, u32[]{:S(2)}) collective-permute-start(bf16[32,2048]{1,0:T(8,128)(2,1)S(1)} %get-tuple-element.961), channel_id=1, source_target_pairs={{4,0},{8,4},{12,8},{16,12},{20,16},{24,20},{28,24},{5,1},{9,5},{13... | collective-permute-start | bytes 393224 | tf_op jit(solution)/shard_map/while/body/eval_jaxpr/ppermute | solution.py:12
  241.3 7.2 %collective-permute-start = (bf16[32,2048]{1,0:T(8,128)(2,1)S(1)}, bf16[32,2048]{1,0:T(8,128)(2,1)S(1)}, u32[]{:S(2)}, u32[]{:S(2)}) collective-permute-start(bf16[32,2048]{1,0:T(8,128)(2,1)S(1)} %get-tuple-element.960), channel_id=1, source_target_pairs={{4,0},{8,4},{12,8},{16,12},{20,16},{24,20},{28,24},{5,1},{9,5},{13... | collective-permute-start | bytes 393224 | tf_op jit(solution)/shard_map/while/body/eval_jaxpr/ppermute | solution.py:12
  242.6 7.8 %collective-permute-start.1 = (bf16[32,2048]{1,0:T(8,128)(2,1)S(1)}, bf16[32,2048]{1,0:T(8,128)(2,1)S(1)}, u32[]{:S(2)}, u32[]{:S(2)}) collective-permute-start(bf16[32,2048]{1,0:T(8,128)(2,1)S(1)} %get-tuple-element.961), channel_id=1, source_target_pairs={{4,0},{8,4},{12,8},{16,12},{20,16},{24,20},{28,24},{5,1},{9,5},{13... | collective-permute-start | bytes 393224 | tf_op jit(solution)/shard_map/while/body/eval_jaxpr/ppermute | solution.py:12
  259.2 3.9 %collective-permute-start.1 = (bf16[32,2048]{1,0:T(8,128)(2,1)S(1)}, bf16[32,2048]{1,0:T(8,128)(2,1)S(1)}, u32[]{:S(2)}, u32[]{:S(2)}) collective-permute-start(bf16[32,2048]{1,0:T(8,128)(2,1)S(1)} %get-tuple-element.961), channel_id=1, source_target_pairs={{4,0},{8,4},{12,8},{16,12},{20,16},{24,20},{28,24},{5,1},{9,5},{13... | collective-permute-start | bytes 393224 | tf_op jit(solution)/shard_map/while/body/eval_jaxpr/ppermute | solution.py:12
  266.1 89.2 %reduce-scatter.3.cloned.1.call-start = ((), (), s32[]{:S(2)}) async-start(), calls=%async_computation.2 | async-start | bytes 2621440 | tf_op jit(solution)/shard_map/reduce_scatter | solution.py:163
  (8 other events, 162.7 us)
Sparse Core Ops, SparseCore 0:
  9.6 48.3 all-gather.4
  59.5 44.4 all-gather.6
  266.2 44.3 reduce-scatter.4
  312.8 42.4 reduce-scatter.2
where the time goes:
time: 365 us; the launch traced here: 364 us
  waiting for transfers between devices  268 us (73%)
  starting transfers between devices  28.5 us (8%)
  other arithmetic  22.8 us (6%)
  matrix products  16.5 us (5%)
  between operations  13.8 us (4%)
  blocking collectives  10.8 us (3%)
    ppermute x22, waiting for transfers between devices, from_behind(): return lax.ppermute(array, axis, pairs)  97 us
    all_gather x1, waiting for transfers between devices, shards(): lax.all_gather(g_weight[0], 'dp', axis=0, tiled=True)  49.2 us
    all_gather x1, waiting for transfers between devices, shards(): lax.all_gather(f_weight[0], 'dp', axis=0, tiled=True)  46.1 us
    reduce_scatter x1, waiting for transfers between devices, shards(): lax.psum_scatter(first_part.astype(jnp.bfloat16), 'dp', scatter_dimension...  42.6 us
    reduce_scatter x1, waiting for transfers between devices, shards(): lax.psum_scatter(second_part.astype(jnp.bfloat16), 'dp', scatter_dimensio...  31.6 us
    ppermute x22, starting transfers between devices, from_behind(): return lax.ppermute(array, axis, pairs)  28.4 us
    psum x1, blocking collectives, shards(): gain_total = lax.psum(gain_acc, 'dp')  10.8 us
  transfers between devices with their start and end apart: 26, of which 26 were waited for; matrix products, arithmetic and copies ran while one was open for 1% of the time, Pallas kernels for 0%

commit v1 on v0

v1 whole, which is shorter than its diff:
```python
import functools

import jax
import jax.numpy as jnp
from jax import lax
from jax.experimental import pallas as pl
from jax.experimental.pallas import tpu as pltpu
from jax.sharding import PartitionSpec as P

offset = 0.25
MESH = pl.DeviceIdType.MESH
f32, bf16 = jnp.float32, jnp.bfloat16


def silu_parts(pre_values):
    sigmoid_value = jax.nn.sigmoid(pre_values)
    return (pre_values * sigmoid_value, sigmoid_value * (1.0 + pre_values * (1.0 - sigmoid_value)))


def inverse_scale(values):
    return lax.rsqrt(jnp.mean(values * values, axis=-1, keepdims=True) + offset)


def kernel(
    n, sections, blocks,
    pair_ref, grad_ref, fw_ref, gw_ref, gains_ref,
    in_pair_ref, in_grad_ref, f_out, g_out, gain_out,
    wf, wg, rx, tx, held, slopes, norms_own, norms, deltas, gain_parts,
    own_sem, w_send, w_recv, p_send, p_recv, n_send, n_recv, d_send, d_recv, c_send, c_recv, out_sem,
):
    s, d = lax.axis_index("section"), lax.axis_index("dp")
    is_last = s == sections - 1
    has_below = s > 0
    not_last = jnp.logical_not(is_last)
    tokens = pair_ref.shape[0]
    h = pair_ref.shape[1] // 2
    part = fw_ref.shape[0]
    rows_per = tokens // blocks

    def peer(k):
        return lax.rem(d + k, n)

    barrier = pltpu.get_barrier_semaphore()
    for k in range(1, n):
        pl.semaphore_signal(barrier, inc=1, device_id=(s, peer(k)), device_id_type=MESH)

    @pl.when(has_below)
    def _():
        pl.semaphore_signal(barrier, inc=1, device_id=(s - 1, d), device_id_type=MESH)

    @pl.when(not_last)
    def _():
        pl.semaphore_signal(barrier, inc=1, device_id=(s + 1, d), device_id_type=MESH)

    neighbours = n - 1 + has_below.astype(jnp.int32) + not_last.astype(jnp.int32)
    pl.semaphore_wait(barrier, neighbours)

    fulls, owns = (wg, wf), (gw_ref, fw_ref)

    def shard(a, owner):
        return fulls[a].at[pl.ds(pl.multiple_of(owner * part, part), part)]

    def hop(a, way, k):
        owner = d - k if way == 0 else d + k
        src = owns[a] if k == 0 else shard(a, owner)
        return pltpu.make_async_remote_copy(
            src_ref=src, dst_ref=shard(a, owner),
            send_sem=w_send.at[a, way, k], recv_sem=w_recv.at[a, way, k],
            device_id=(s, d + 1 if way == 0 else d - 1), device_id_type=MESH,
        )

    def reach(way, k):
        if way == 0:
            return jnp.logical_and(d - k >= 0, d < n - 1)
        return jnp.logical_and(d + k < n, d > 0)

    def arrives(way, k):
        return d - k >= 0 if way == 0 else d + k < n

    for a in range(2):
        for way in range(2):
            @pl.when(reach(way, 0))
            def _():
                hop(a, way, 0).start()
    own_copies = [pltpu.make_async_copy(owns[a], shard(a, d), own_sem.at[a]) for a in range(2)]
    for copy in own_copies:
        copy.start()
    for k in range(1, n):
        for a in range(2):
            for way in range(2):
                @pl.when(arrives(way, k))
                def _():
                    owner = d - k if way == 0 else d + k
                    pltpu.make_async_remote_copy(
                        src_ref=owns[a], dst_ref=shard(a, owner),
                        send_sem=w_send.at[a, way, k - 1], recv_sem=w_recv.at[a, way, k - 1],
                        device_id=(s, d - 1 if way == 0 else d + 1), device_id_type=MESH,
                    ).wait_recv()

                if k < n - 1:
                    @pl.when(reach(way, k))
                    def _():
                        hop(a, way, k).start()
    for copy in own_copies:
        copy.wait()

    gain_out[...] = jnp.zeros_like(gain_out)

    def pair_copy(i, b):
        rows = pl.ds(pl.multiple_of(b * rows_per, rows_per), rows_per)
        return pltpu.make_async_remote_copy(
            src_ref=tx.at[i, rows], dst_ref=rx.at[i, rows],
            send_sem=p_send.at[i], recv_sem=p_recv.at[i, b],
            device_id=(s - 1, d), device_id_type=MESH,
        )

    def take(i, b, rows, source, column):
        @pl.when(is_last)
        def _():
            held[i] = source[rows, column].astype(f32)

        @pl.when(not_last)
        def _():
            rows_ = pl.ds(pl.multiple_of(b * rows_per, rows_per), rows_per)
            pltpu.make_async_remote_copy(
                src_ref=tx.at[i, rows_], dst_ref=rx.at[i, rows_],
                send_sem=p_send.at[i], recv_sem=p_recv.at[i, b],
                device_id=(s + 1, d), device_id_type=MESH,
            ).wait_recv()
            held[i] = rx[i, rows].astype(f32)

    def give(i, b, rows, values):
        tx[i, rows] = values.astype(bf16)

        @pl.when(has_below)
        def _():
            pair_copy(i, b).start()

    def share_norm(a, rows, normed):
        for e in range(n):
            norms_own[a, e, rows] = normed[:, e * part:(e + 1) * part]
        for k in range(1, n):
            e = peer(k)
            pltpu.make_async_remote_copy(
                src_ref=norms_own.at[a, e, rows], dst_ref=norms.at[a, d, rows],
                send_sem=n_send.at[a], recv_sem=n_recv.at[a],
                device_id=(s, e), device_id_type=MESH,
            ).start()

    def share_delta(a, rows, delta):
        deltas[a, d, rows] = delta
        for k in range(1, n):
            pltpu.make_async_remote_copy(
                src_ref=deltas.at[a, d, rows], dst_ref=deltas.at[a, d, rows],
                send_sem=d_send.at[a], recv_sem=d_recv.at[a],
                device_id=(s, peer(k)), device_id_type=MESH,
            ).start()

    first, second = pl.ds(0, h), pl.ds(h, h)
    trans = (((1,), (1,)), ((), ()))

    def block(b, carry):
        rows = pl.ds(pl.multiple_of(b * rows_per, rows_per), rows_per)
        gain_f, gain_g = gains_ref[0:1, :], gains_ref[1:2, :]
        take(0, b, rows, pair_ref, first)
        y1 = held[0]
        r1 = inverse_scale(y1)
        norm_g = (y1 * r1 * gain_g).astype(bf16)
        pre_g = jnp.dot(norm_g, wg[...], preferred_element_type=f32)
        take(1, b, rows, pair_ref, second)
        act_g, slope_g = silu_parts(pre_g)
        x2 = held[1] - act_g
        in_pair_ref[rows, second] = x2
        give(1, b, rows, x2)
        slopes[0] = slope_g
        r2 = inverse_scale(x2)
        norm_f = (x2 * r2 * gain_f).astype(bf16)
        pre_f = jnp.dot(norm_f, wf[...], preferred_element_type=f32)
        act_f, slope_f = silu_parts(pre_f)
        x1 = held[0] - act_f
        in_pair_ref[rows, first] = x1
        give(0, b, rows, x1)
        slopes[1] = slope_f
        share_norm(0, rows, norm_f)
        share_norm(1, rows, norm_g)

        take(3, b, rows, grad_ref, second)
        take(2, b, rows, grad_ref, first)
        delta_g = (held[3] * slopes[0]).astype(bf16)
        back_g = lax.dot_general(delta_g, wg[...], trans, preferred_element_type=f32)
        share_delta(1, rows, delta_g)
        y1 = held[0]
        weighted = gain_g * back_g
        gz = held[2] + r1 * weighted - y1 * (r1 * r1 * r1) * jnp.mean(
            weighted * y1, axis=-1, keepdims=True
        )
        in_grad_ref[rows, first] = gz.astype(bf16)
        give(2, b, rows, gz)
        gain_out[1:2, :] += jnp.sum(back_g * y1 * r1, axis=0, keepdims=True)
        delta_f = (gz * slopes[1]).astype(bf16)
        back_f = lax.dot_general(delta_f, wf[...], trans, preferred_element_type=f32)
        share_delta(0, rows, delta_f)
        x2 = in_pair_ref[rows, second]
        weighted = gain_f * back_f
        gx2 = held[3] + r2 * weighted - x2 * (r2 * r2 * r2) * jnp.mean(
            weighted * x2, axis=-1, keepdims=True
        )
        in_grad_ref[rows, second] = gx2.astype(bf16)
        give(3, b, rows, gx2)
        gain_out[0:1, :] += jnp.sum(back_f * x2 * r2, axis=0, keepdims=True)
        return carry

    lax.fori_loop(0, blocks, block, 0)

    gain_parts[d] = gain_out[...]
    for k in range(1, n):
        pltpu.make_async_remote_copy(
            src_ref=gain_parts.at[d], dst_ref=gain_parts.at[d],
            send_sem=c_send, recv_sem=c_recv,
            device_id=(s, peer(k)), device_id_type=MESH,
        ).start()

    def wait_bytes(ref, sem):
        pltpu.make_async_copy(ref, ref, sem).wait()

    for a in range(2):
        norms[a, d] = norms_own[a, d]
    others = pl.ds(0, n - 1)
    for a, out in ((1, g_out), (0, f_out)):
        wait_bytes(norms.at[a, others], n_recv.at[a])
        wait_bytes(deltas.at[a, others], d_recv.at[a])
        out[...] = lax.dot_general(
            norms[a].reshape(n * tokens, part), deltas[a].reshape(n * tokens, h),
            (((0,), (0,)), ((), ())), preferred_element_type=f32,
        )
    wait_bytes(gain_parts.at[others], c_recv)
    total = gain_parts[0]
    for e in range(1, n):
        total = total + gain_parts[e]
    gain_out[...] = total

    for a in range(2):
        wait_bytes(norms.at[a, others], n_send.at[a])
        wait_bytes(deltas.at[a, others], d_send.at[a])
    wait_bytes(gain_parts.at[others], c_send)

    @pl.when(has_below)
    def _():
        for i in range(4):
            wait_bytes(tx.at[i], p_send.at[i])

    for k in range(n - 1):
        for a in range(2):
            for way in range(2):
                @pl.when(reach(way, k))
                def _():
                    hop(a, way, k).wait_send()


def shards(out_pair, out_grad, f_weight, g_weight, gains):
    n, sections = lax.axis_size("dp"), lax.axis_size("section")
    tokens, width = out_pair.shape
    h = width // 2
    part = f_weight.shape[1]
    blocks = 4
    vmem = pl.BlockSpec(memory_space=pltpu.VMEM)
    dma = pltpu.SemaphoreType.DMA
    outs = pl.pallas_call(
        functools.partial(kernel, n, sections, blocks),
        out_shape=(
            jax.ShapeDtypeStruct((tokens, width), f32),
            jax.ShapeDtypeStruct((tokens, width), bf16),
            jax.ShapeDtypeStruct((part, h), f32),
            jax.ShapeDtypeStruct((part, h), f32),
            jax.ShapeDtypeStruct((2, h), f32),
        ),
        in_specs=[vmem] * 5,
        out_specs=[vmem] * 5,
        scratch_shapes=[
            pltpu.VMEM((h, h), bf16),
            pltpu.VMEM((h, h), bf16),
            pltpu.VMEM((4, tokens, h), bf16),
            pltpu.VMEM((4, tokens, h), bf16),
            pltpu.VMEM((4, tokens // blocks, h), f32),
            pltpu.VMEM((2, tokens // blocks, h), f32),
            pltpu.VMEM((2, n, tokens, part), bf16),
            pltpu.VMEM((2, n, tokens, part), bf16),
            pltpu.VMEM((2, n, tokens, h), bf16),
            pltpu.VMEM((n, 2, h), f32),
            dma((2,)),
            dma((2, 2, n)),
            dma((2, 2, n)),
            dma((4,)),
            dma((4, blocks)),
            dma((2,)),
            dma((2,)),
            dma((2,)),
            dma((2,)),
            dma,
            dma,
            dma,
        ],
        compiler_params=pltpu.CompilerParams(
            collective_id=0, has_side_effects=True, vmem_limit_bytes=60 * 1024 * 1024
        ),
    )(out_pair, out_grad, f_weight[0], g_weight[0], gains[0])
    return tuple(out[None] for out in outs)


def solution(mesh):
    placed = (
        P("dp", None),
        P("dp", None),
        P("section", "dp", None),
        P("section", "dp", None),
        P("section", None, None),
    )
    return jax.shard_map(
        shards,
        mesh=mesh,
        in_specs=placed,
        out_specs=(
            P("section", "dp", None),
            P("section", "dp", None),
            P("section", "dp", None),
            P("section", "dp", None),
            P("section", None, None),
        ),
        check_vma=False,
    )
```

time: 365 us -> 166 us (0.45)
  waiting for transfers between devices: 268 us -> 0 us
  Pallas kernels: 0 us -> 159 us
  starting transfers between devices: 28.5 us -> 0 us
  other arithmetic: 22.8 us -> 0 us
  matrix products: 16.5 us -> 0 us
  between operations: 13.8 us -> 0.66 us
  blocking collectives: 10.8 us -> 0 us
    pallas_call x0 -> x1, Pallas kernels: none -> 159 us  [shards(): pl.pallas_call(functools.partial(kernel, n, sections, blocks), out_shape=...]
    ppermute x22 -> x0, waiting for transfers between devices: 97 us -> none  [from_behind(): return lax.ppermute(array, axis, pairs)]
    all_gather x2 -> x0, waiting for transfers between devices: 95.3 us -> none  [the longest x1 49.2 us: shards(): lax.all_gather(g_weight[0], 'dp', axis=0, tiled=True)]
    reduce_scatter x2 -> x0, waiting for transfers between devices: 74.2 us -> none  [the longest x1 42.6 us: shards(): lax.psum_scatter(first_part.astype(jnp.bfloat16), 'dp', scatter_dimension...]
    ppermute x22 -> x0, starting transfers between devices: 28.4 us -> none  [from_behind(): return lax.ppermute(array, axis, pairs)]
    dot_general x18 -> x0, matrix products: 16.5 us -> none  [the longest x8 6.82 us: times_transposed(): lax.dot_general(delta, weight_full, (((1,), (1,)), ((), ())), preferred_e...]
    psum x1 -> x0, blocking collectives: 10.8 us -> none  [shards(): gain_total = lax.psum(gain_acc, 'dp')]
    dynamic_update_slice x12 -> x0, other arithmetic: 8.91 us -> none  [the longest x4 3.29 us: compute(): lax.dynamic_update_slice_in_dim(first_deltas, results[5], row_start, 0)]
  transfers between devices with their start and end apart: 26 -> 0, of which waited for: 26 -> 0; matrix products, arithmetic and copies ran while one was open for 1% -> 0% of each run, Pallas kernels for 0% -> 0%
where the time goes in v1:
time: 166 us
  Pallas kernels  159 us (96%)
  local copies, waits for them, and re-layouts  6.39 us (4%)
    pallas_call x1, Pallas kernels, shards(): pl.pallas_call(functools.partial(kernel, n, sections, blocks), out_shape=...  159 us
    unnamed x13, local copies, waits for them, and re-layouts  6.39 us

profile of v1, /device:TPU:0, one launch (start us, length us, event | category | flops | bytes accessed | tf_op | source)
XLA Modules:
  0.0 166.0 jit_solution(11030910459190628200)
XLA Ops:
  0.6 158.9 %shard_map.92 = (f32[128,2048]{1,0:T(8,128)}, bf16[128,2048]{1,0:T(8,128)(2,1)}, f32[256,1024]{1,0:T(8,128)}, f32[256,1024]{1,0:T(8,128)}, f32[2,1024]{1,0:T(2,128)}) custom-call(f32[128,2048]{1,0:T(8,128)} %pair_ref.1, bf16[128,2048]{1,0:T(8,128)(2,1)} %grad_ref.1, bf16[256,1024]{1,0:T(8,128)(2,1)} %bitcast.11, bf16[256,1024]{1,0:T(8,128)(2,1)} %bitcast.12, ...), custom_call_target="tpu_custom_call" | custom-call | tf_op jit(solution)/shard_map/pallas_call | solution.py:268
  159.6 0.0 copy-start.2
  159.6 0.0 copy-start.1
  159.6 2.4 %copy.15 = f32[1,128,2048]{2,1,0:T(8,128)} copy(f32[1,128,2048]{2,1,0:T(8,128)} %bitcast.10) | data formatting | bytes 2097152
  162.0 0.0 copy-done.2
  162.0 0.8 copy.16
  162.8 0.0 copy-done.1
  162.8 0.0 copy-start
  162.8 1.0 copy.17
  163.8 0.6 copy-done
  164.4 0.0 copy-start.3
  164.4 1.0 copy.18
  165.4 0.0 copy-done.3
  165.4 0.6 copy.19
Async XLA Ops:
  159.6 2.4 %copy-start.2 = (bf16[128,2048]{1,0:T(8,128)(2,1)S(1)}, bf16[128,2048]{1,0:T(8,128)(2,1)}, u32[]{:S(2)}) copy-start(bf16[128,2048]{1,0:T(8,128)(2,1)} %get-tuple-element.11) | copy-start | bytes 1572868
  159.6 3.2 %copy-start.1 = (f32[256,1024]{1,0:T(8,128)S(1)}, f32[256,1024]{1,0:T(8,128)}, u32[]{:S(2)}) copy-start(f32[256,1024]{1,0:T(8,128)} %get-tuple-element.12) | copy-start | bytes 3145732
  162.8 1.6 copy-start
  164.4 1.0 copy-start.3

commit v2 on v1

--- a/solution.py
+++ b/solution.py
@@ -26,7 +26,7 @@
     pair_ref, grad_ref, fw_ref, gw_ref, gains_ref,
     in_pair_ref, in_grad_ref, f_out, g_out, gain_out,
     wf, wg, rx, tx, held, slopes, norms_own, norms, deltas, gain_parts,
-    own_sem, w_send, w_recv, p_send, p_recv, n_send, n_recv, d_send, d_recv, c_send, c_recv, out_sem,
+    own_sem, w_send, w_recv, p_send, p_recv, n_send, n_recv, d_send, d_recv, c_send, c_recv,
 ):
     s, d = lax.axis_index("section"), lax.axis_index("dp")
     is_last = s == sections - 1
@@ -147,14 +147,20 @@
                 device_id=(s, e), device_id_type=MESH,
             ).start()
 
+    def delta_hop(a, way, k, rows):
+        owner = d - k if way == 0 else d + k
+        return pltpu.make_async_remote_copy(
+            src_ref=deltas.at[a, owner, rows], dst_ref=deltas.at[a, owner, rows],
+            send_sem=d_send.at[a, way, k], recv_sem=d_recv.at[a, way, k],
+            device_id=(s, d + 1 if way == 0 else d - 1), device_id_type=MESH,
+        )
+
     def share_delta(a, rows, delta):
         deltas[a, d, rows] = delta
-        for k in range(1, n):
-            pltpu.make_async_remote_copy(
-                src_ref=deltas.at[a, d, rows], dst_ref=deltas.at[a, d, rows],
-                send_sem=d_send.at[a], recv_sem=d_recv.at[a],
-                device_id=(s, peer(k)), device_id_type=MESH,
-            ).start()
+        for way in range(2):
+            @pl.when(reach(way, 0))
+            def _():
+                delta_hop(a, way, 0, rows).start()
 
     first, second = pl.ds(0, h), pl.ds(h, h)
     trans = (((1,), (1,)), ((), ()))
@@ -225,14 +231,24 @@
 
     for a in range(2):
         norms[a, d] = norms_own[a, d]
-    others = pl.ds(0, n - 1)
-    for a, out in ((1, g_out), (0, f_out)):
-        wait_bytes(norms.at[a, others], n_recv.at[a])
-        wait_bytes(deltas.at[a, others], d_recv.at[a])
-        out[...] = lax.dot_general(
-            norms[a].reshape(n * tokens, part), deltas[a].reshape(n * tokens, h),
-            (((0,), (0,)), ((), ())), preferred_element_type=f32,
-        )
+    others, whole = pl.ds(0, n - 1), pl.ds(0, tokens)
+    for k in range(1, n):
+        for a, out in ((1, g_out), (0, f_out)):
+            for way in range(2):
+                @pl.when(arrives(way, k))
+                def _():
+                    wait_bytes(deltas.at[a, d - k if way == 0 else d + k], d_recv.at[a, way, k - 1])
+
+                if k < n - 1:
+                    @pl.when(reach(way, k))
+                    def _():
+                        delta_hop(a, way, k, whole).start()
+            if k == n - 1:
+                wait_bytes(norms.at[a, others], n_recv.at[a])
+                out[...] = lax.dot_general(
+                    norms[a].reshape(n * tokens, part), deltas[a].reshape(n * tokens, h),
+                    (((0,), (0,)), ((), ())), preferred_element_type=f32,
+                )
     wait_bytes(gain_parts.at[others], c_recv)
     total = gain_parts[0]
     for e in range(1, n):
@@ -241,7 +257,11 @@
 
     for a in range(2):
         wait_bytes(norms.at[a, others], n_send.at[a])
-        wait_bytes(deltas.at[a, others], d_send.at[a])
+        for k in range(n - 1):
+            for way in range(2):
+                @pl.when(reach(way, k))
+                def _():
+                    wait_bytes(deltas.at[a, d - k if way == 0 else d + k], d_send.at[a, way, k])
     wait_bytes(gain_parts.at[others], c_send)
 
     @pl.when(has_below)
@@ -294,9 +314,8 @@
             dma((4, blocks)),
             dma((2,)),
             dma((2,)),
-            dma((2,)),
-            dma((2,)),
-            dma,
+            dma((2, 2, n)),
+            dma((2, 2, n)),
             dma,
             dma,
         ],

time: 166 us -> 154 us (0.928)
  Pallas kernels: 159 us -> 147 us
    pallas_call x1, Pallas kernels: 159 us -> 147 us  [shards(): pl.pallas_call(functools.partial(kernel, n, sections, blocks), out_shape=...]
where the time goes in v2:
time: 154 us
  Pallas kernels  147 us (95%)
  local copies, waits for them, and re-layouts  6.39 us (4%)
    pallas_call x1, Pallas kernels, shards(): pl.pallas_call(functools.partial(kernel, n, sections, blocks), out_shape=...  147 us
    unnamed x13, local copies, waits for them, and re-layouts  6.39 us

profile of v2, /device:TPU:0, one launch (start us, length us, event | category | flops | bytes accessed | tf_op | source)
XLA Modules:
  0.0 153.7 jit_solution(13409134990500391472)
XLA Ops:
  0.6 146.7 %shard_map.92 = (f32[128,2048]{1,0:T(8,128)}, bf16[128,2048]{1,0:T(8,128)(2,1)}, f32[256,1024]{1,0:T(8,128)}, f32[256,1024]{1,0:T(8,128)}, f32[2,1024]{1,0:T(2,128)}) custom-call(f32[128,2048]{1,0:T(8,128)} %pair_ref.1, bf16[128,2048]{1,0:T(8,128)(2,1)} %grad_ref.1, bf16[256,1024]{1,0:T(8,128)(2,1)} %bitcast.11, bf16[256,1024]{1,0:T(8,128)(2,1)} %bitcast.12, ...), custom_call_target="tpu_custom_call" | custom-call | tf_op jit(solution)/shard_map/pallas_call | solution.py:288
  147.3 0.0 copy-start.2
  147.3 0.0 copy-start.1
  147.4 2.4 %copy.15 = f32[1,128,2048]{2,1,0:T(8,128)} copy(f32[1,128,2048]{2,1,0:T(8,128)} %bitcast.10) | data formatting | bytes 2097152
  149.8 0.0 copy-done.2
  149.8 0.8 copy.16
  150.6 0.0 copy-done.1
  150.6 0.0 copy-start
  150.6 1.0 copy.17
  151.5 0.6 copy-done
  152.2 0.0 copy-start.3
  152.2 1.0 copy.18
  153.1 0.0 copy-done.3
  153.1 0.6 copy.19
Async XLA Ops:
  147.3 2.4 %copy-start.2 = (bf16[128,2048]{1,0:T(8,128)(2,1)S(1)}, bf16[128,2048]{1,0:T(8,128)(2,1)}, u32[]{:S(2)}) copy-start(bf16[128,2048]{1,0:T(8,128)(2,1)} %get-tuple-element.11) | copy-start | bytes 1572868
  147.3 3.2 %copy-start.1 = (f32[256,1024]{1,0:T(8,128)S(1)}, f32[256,1024]{1,0:T(8,128)}, u32[]{:S(2)}) copy-start(f32[256,1024]{1,0:T(8,128)} %get-tuple-element.12) | copy-start | bytes 3145732
  150.6 1.6 %copy-start = (f32[256,1024]{1,0:T(8,128)S(1)}, f32[256,1024]{1,0:T(8,128)}, u32[]{:S(2)}) copy-start(f32[256,1024]{1,0:T(8,128)} %get-tuple-element.13) | copy-start | bytes 3145732
  152.2 1.0 copy-start.3

commit v3 on v2

--- a/solution.py
+++ b/solution.py
@@ -25,8 +25,8 @@
     n, sections, blocks,
     pair_ref, grad_ref, fw_ref, gw_ref, gains_ref,
     in_pair_ref, in_grad_ref, f_out, g_out, gain_out,
-    wf, wg, rx, tx, held, slopes, norms_own, norms, deltas, gain_parts,
-    own_sem, w_send, w_recv, p_send, p_recv, n_send, n_recv, d_send, d_recv, c_send, c_recv,
+    wf, wg, wft, wgt, aside, rx, tx, held, slopes, norms_own, norms, deltas, gain_parts,
+    own_sem, i_send, i_recv, h_send, h_recv, o_send, o_recv, w_send, w_recv, p_send, p_recv, n_send, n_recv, d_send, d_recv, c_send, c_recv,
 ):
     s, d = lax.axis_index("section"), lax.axis_index("dp")
     is_last = s == sections - 1
@@ -52,22 +52,61 @@
     def _():
         pl.semaphore_signal(barrier, inc=1, device_id=(s + 1, d), device_id_type=MESH)
 
-    neighbours = n - 1 + has_below.astype(jnp.int32) + not_last.astype(jnp.int32)
+    half = sections // 2
+    partner = lax.rem(s + half, sections)
+    high, low = s >= half, s < half
+    pl.semaphore_signal(barrier, inc=1, device_id=(partner, d), device_id_type=MESH)
+    neighbours = n + has_below.astype(jnp.int32) + not_last.astype(jnp.int32)
     pl.semaphore_wait(barrier, neighbours)
 
-    fulls, owns = (wg, wf), (gw_ref, fw_ref)
-
-    def shard(a, owner):
-        return fulls[a].at[pl.ds(pl.multiple_of(owner * part, part), part)]
-
-    def hop(a, way, k):
-        owner = d - k if way == 0 else d + k
-        src = owns[a] if k == 0 else shard(a, owner)
-        return pltpu.make_async_remote_copy(
-            src_ref=src, dst_ref=shard(a, owner),
+    fulls, owns, turned = (wg, wf), (gw_ref, fw_ref), (wgt, wft)
+    keep = h - aside.shape[3]
+    variants = ((low, pl.ds(0, h)), (high, pl.ds(0, keep)))
+    rest = pl.ds(keep, h - keep)
+
+    def shard(a, owner, cols):
+        return fulls[a].at[pl.ds(pl.multiple_of(owner * part, part), part), cols]
+
+    def owner_of(way, k):
+        return d - k if way == 0 else d + k
+
+    def ahead(way):
+        return d + 1 if way == 0 else d - 1
+
+    def hop(a, way, k, cols):
+        owner = owner_of(way, k)
+        src = owns[a].at[:, cols] if k == 0 else shard(a, owner, cols)
+        return pltpu.make_async_remote_copy(
+            src_ref=src, dst_ref=shard(a, owner, cols),
             send_sem=w_send.at[a, way, k], recv_sem=w_recv.at[a, way, k],
-            device_id=(s, d + 1 if way == 0 else d - 1), device_id_type=MESH,
-        )
+            device_id=(s, ahead(way)), device_id_type=MESH,
+        )
+
+    def aside_in(a):
+        return pltpu.make_async_remote_copy(
+            src_ref=owns[a].at[:, rest], dst_ref=aside.at[a, d],
+            send_sem=i_send.at[a], recv_sem=i_recv.at[a],
+            device_id=(partner, d), device_id_type=MESH,
+        )
+
+    def aside_hop(a, way, k):
+        owner = owner_of(way, k)
+        return pltpu.make_async_remote_copy(
+            src_ref=aside.at[a, owner], dst_ref=aside.at[a, owner],
+            send_sem=h_send.at[a, way, k], recv_sem=h_recv.at[a, way, k],
+            device_id=(s, ahead(way)), device_id_type=MESH,
+        )
+
+    def aside_out(a, way, k):
+        owner = owner_of(way, k)
+        return pltpu.make_async_remote_copy(
+            src_ref=aside.at[a, owner], dst_ref=shard(a, owner, rest),
+            send_sem=o_send.at[a, way, k], recv_sem=o_recv.at[a, way, k],
+            device_id=(partner, d), device_id_type=MESH,
+        )
+
+    def wait_bytes(ref, sem):
+        pltpu.make_async_copy(ref, ref, sem).wait()
 
     def reach(way, k):
         if way == 0:
@@ -77,32 +116,78 @@
     def arrives(way, k):
         return d - k >= 0 if way == 0 else d + k < n
 
+    both = jnp.logical_and
+
+    @pl.when(high)
+    def _():
+        for a in range(2):
+            aside_in(a).start()
+
+    @pl.when(low)
+    def _():
+        for a in range(2):
+            wait_bytes(aside.at[a, d], i_recv.at[a])
+            for way in range(2):
+                @pl.when(reach(way, 0))
+                def _():
+                    aside_hop(a, way, 0).start()
+
     for a in range(2):
         for way in range(2):
-            @pl.when(reach(way, 0))
-            def _():
-                hop(a, way, 0).start()
-    own_copies = [pltpu.make_async_copy(owns[a], shard(a, d), own_sem.at[a]) for a in range(2)]
+            for side, cols in variants:
+                @pl.when(both(side, reach(way, 0)))
+                def _():
+                    hop(a, way, 0, cols).start()
+    early = part % 128 == 0
+
+    def turn(a, owner):
+        span = pl.ds(pl.multiple_of(owner * part, part), part)
+        turned[a][:, span] = fulls[a][span, :].T
+
+    own_copies = [
+        pltpu.make_async_copy(owns[a], shard(a, d, pl.ds(0, h)), own_sem.at[a]) for a in range(2)
+    ]
     for copy in own_copies:
         copy.start()
+    for a, copy in enumerate(own_copies):
+        copy.wait()
+        if early:
+            turn(a, d)
     for k in range(1, n):
         for a in range(2):
             for way in range(2):
-                @pl.when(arrives(way, k))
-                def _():
-                    owner = d - k if way == 0 else d + k
-                    pltpu.make_async_remote_copy(
-                        src_ref=owns[a], dst_ref=shard(a, owner),
-                        send_sem=w_send.at[a, way, k - 1], recv_sem=w_recv.at[a, way, k - 1],
-                        device_id=(s, d - 1 if way == 0 else d + 1), device_id_type=MESH,
-                    ).wait_recv()
-
-                if k < n - 1:
-                    @pl.when(reach(way, k))
+                @pl.when(both(low, arrives(way, k)))
+                def _():
+                    wait_bytes(aside.at[a, owner_of(way, k)], h_recv.at[a, way, k - 1])
+                    if k < n - 1:
+                        @pl.when(reach(way, k))
+                        def _():
+                            aside_hop(a, way, k).start()
+                    aside_out(a, way, k).start()
+        for a in range(2):
+            for way in range(2):
+                for side, cols in variants:
+                    @pl.when(both(side, arrives(way, k)))
                     def _():
-                        hop(a, way, k).start()
-    for copy in own_copies:
-        copy.wait()
+                        wait_bytes(shard(a, owner_of(way, k), cols), w_recv.at[a, way, k - 1])
+
+                    if k < n - 1:
+                        @pl.when(both(side, reach(way, k)))
+                        def _():
+                            hop(a, way, k, cols).start()
+        for a in range(2):
+            for way in range(2):
+                @pl.when(both(high, arrives(way, k)))
+                def _():
+                    wait_bytes(shard(a, owner_of(way, k), rest), o_recv.at[a, way, k])
+
+                if early:
+                    @pl.when(arrives(way, k))
+                    def _():
+                        turn(a, owner_of(way, k))
+    if not early:
+        for a in range(2):
+            turned[a][...] = fulls[a][...].T
 
     gain_out[...] = jnp.zeros_like(gain_out)
 
@@ -163,7 +248,6 @@
                 delta_hop(a, way, 0, rows).start()
 
     first, second = pl.ds(0, h), pl.ds(h, h)
-    trans = (((1,), (1,)), ((), ()))
 
     def block(b, carry):
         rows = pl.ds(pl.multiple_of(b * rows_per, rows_per), rows_per)
@@ -193,7 +277,7 @@
         take(3, b, rows, grad_ref, second)
         take(2, b, rows, grad_ref, first)
         delta_g = (held[3] * slopes[0]).astype(bf16)
-        back_g = lax.dot_general(delta_g, wg[...], trans, preferred_element_type=f32)
+        back_g = jnp.dot(delta_g, wgt[...], preferred_element_type=f32)
         share_delta(1, rows, delta_g)
         y1 = held[0]
         weighted = gain_g * back_g
@@ -204,7 +288,7 @@
         give(2, b, rows, gz)
         gain_out[1:2, :] += jnp.sum(back_g * y1 * r1, axis=0, keepdims=True)
         delta_f = (gz * slopes[1]).astype(bf16)
-        back_f = lax.dot_general(delta_f, wf[...], trans, preferred_element_type=f32)
+        back_f = jnp.dot(delta_f, wft[...], preferred_element_type=f32)
         share_delta(0, rows, delta_f)
         x2 = in_pair_ref[rows, second]
         weighted = gain_f * back_f
@@ -225,9 +309,6 @@
             send_sem=c_send, recv_sem=c_recv,
             device_id=(s, peer(k)), device_id_type=MESH,
         ).start()
-
-    def wait_bytes(ref, sem):
-        pltpu.make_async_copy(ref, ref, sem).wait()
 
     for a in range(2):
         norms[a, d] = norms_own[a, d]
@@ -269,12 +350,27 @@
         for i in range(4):
             wait_bytes(tx.at[i], p_send.at[i])
 
-    for k in range(n - 1):
-        for a in range(2):
-            for way in range(2):
-                @pl.when(reach(way, k))
-                def _():
-                    hop(a, way, k).wait_send()
+    @pl.when(high)
+    def _():
+        for a in range(2):
+            aside_in(a).wait_send()
+
+    for k in range(n):
+        for a in range(2):
+            for way in range(2):
+                if k < n - 1:
+                    for side, cols in variants:
+                        @pl.when(both(side, reach(way, k)))
+                        def _():
+                            hop(a, way, k, cols).wait_send()
+
+                    @pl.when(both(low, reach(way, k)))
+                    def _():
+                        aside_hop(a, way, k).wait_send()
+                if k > 0:
+                    @pl.when(both(low, arrives(way, k)))
+                    def _():
+                        aside_out(a, way, k).wait_send()
 
 
 def shards(out_pair, out_grad, f_weight, g_weight, gains):
@@ -299,6 +395,9 @@
         scratch_shapes=[
             pltpu.VMEM((h, h), bf16),
             pltpu.VMEM((h, h), bf16),
+            pltpu.VMEM((h, h), bf16),
+            pltpu.VMEM((h, h), bf16),
+            pltpu.VMEM((2, n, part, h // 8), bf16),
             pltpu.VMEM((4, tokens, h), bf16),
             pltpu.VMEM((4, tokens, h), bf16),
             pltpu.VMEM((4, tokens // blocks, h), f32),
@@ -308,6 +407,12 @@
             pltpu.VMEM((2, n, tokens, h), bf16),
             pltpu.VMEM((n, 2, h), f32),
             dma((2,)),
+            dma((2,)),
+            dma((2,)),
+            dma((2, 2, n)),
+            dma((2, 2, n)),
+            dma((2, 2, n)),
+            dma((2, 2, n)),
             dma((2, 2, n)),
             dma((2, 2, n)),
             dma((4,)),

time: 154 us -> 152 us (0.987)
  Pallas kernels: 147 us -> 145 us
    pallas_call x1, Pallas kernels: 147 us -> 145 us  [shards(): pl.pallas_call(functools.partial(kernel, n, sections, blocks), out_shape=...]
where the time goes in v3:
time: 152 us
  Pallas kernels  145 us (95%)
  local copies, waits for them, and re-layouts  6.39 us (4%)
    pallas_call x1, Pallas kernels, shards(): pl.pallas_call(functools.partial(kernel, n, sections, blocks), out_shape=...  145 us
    unnamed x13, local copies, waits for them, and re-layouts  6.39 us

profile of v3, /device:TPU:0, one launch (start us, length us, event | category | flops | bytes accessed | tf_op | source)
XLA Modules:
  0.0 152.0 jit_solution(4409991972919812244)
XLA Ops:
  0.6 145.0 %shard_map.92 = (f32[128,2048]{1,0:T(8,128)}, bf16[128,2048]{1,0:T(8,128)(2,1)}, f32[256,1024]{1,0:T(8,128)}, f32[256,1024]{1,0:T(8,128)}, f32[2,1024]{1,0:T(2,128)}) custom-call(f32[128,2048]{1,0:T(8,128)} %pair_ref.1, bf16[128,2048]{1,0:T(8,128)(2,1)} %grad_ref.1, bf16[256,1024]{1,0:T(8,128)(2,1)} %bitcast.11, bf16[256,1024]{1,0:T(8,128)(2,1)} %bitcast.12, ...), custom_call_target="tpu_custom_call" | custom-call | tf_op jit(solution)/shard_map/pallas_call | solution.py:384
  145.6 0.0 copy-start.2
  145.6 0.0 copy-start.1
  145.7 2.4 %copy.15 = f32[1,128,2048]{2,1,0:T(8,128)} copy(f32[1,128,2048]{2,1,0:T(8,128)} %bitcast.10) | data formatting | bytes 2097152
  148.1 0.0 copy-done.2
  148.1 0.8 copy.16
  148.9 0.0 copy-done.1
  148.9 0.0 copy-start
  148.9 1.0 copy.17
  149.8 0.6 copy-done
  150.5 0.0 copy-start.3
  150.5 1.0 copy.18
  151.4 0.0 copy-done.3
  151.4 0.6 copy.19
Async XLA Ops:
  145.6 2.4 %copy-start.2 = (bf16[128,2048]{1,0:T(8,128)(2,1)S(1)}, bf16[128,2048]{1,0:T(8,128)(2,1)}, u32[]{:S(2)}) copy-start(bf16[128,2048]{1,0:T(8,128)(2,1)} %get-tuple-element.11) | copy-start | bytes 1572868
  145.6 3.2 %copy-start.1 = (f32[256,1024]{1,0:T(8,128)S(1)}, f32[256,1024]{1,0:T(8,128)}, u32[]{:S(2)}) copy-start(f32[256,1024]{1,0:T(8,128)} %get-tuple-element.12) | copy-start | bytes 3145732
  148.9 1.6 %copy-start = (f32[256,1024]{1,0:T(8,128)S(1)}, f32[256,1024]{1,0:T(8,128)}, u32[]{:S(2)}) copy-start(f32[256,1024]{1,0:T(8,128)} %get-tuple-element.13) | copy-start | bytes 3145732
  150.5 1.0 copy-start.3

commit v4 on v3

--- a/solution.py
+++ b/solution.py
@@ -25,8 +25,8 @@
     n, sections, blocks,
     pair_ref, grad_ref, fw_ref, gw_ref, gains_ref,
     in_pair_ref, in_grad_ref, f_out, g_out, gain_out,
-    wf, wg, wft, wgt, aside, rx, tx, held, slopes, norms_own, norms, deltas, gain_parts,
-    own_sem, i_send, i_recv, h_send, h_recv, o_send, o_recv, w_send, w_recv, p_send, p_recv, n_send, n_recv, d_send, d_recv, c_send, c_recv,
+    wf, wg, wft, wgt, aside, late, rx, tx, held, slopes, norms_own, norms, deltas, gain_parts,
+    l_sem, lh_send, lh_recv, lo_send, lo_recv, own_sem, i_send, i_recv, h_send, h_recv, o_send, o_recv, w_send, w_recv, p_send, p_recv, n_send, n_recv, d_send, d_recv, c_send, c_recv,
 ):
     s, d = lax.axis_index("section"), lax.axis_index("dp")
     is_last = s == sections - 1
@@ -232,10 +232,39 @@
                 device_id=(s, e), device_id_type=MESH,
             ).start()
 
-    def delta_hop(a, way, k, rows):
+    split = h - late.shape[2]
+    tail = pl.ds(split, h - split)
+    delta_variants = (
+        ((jnp.bool_(True), pl.ds(0, h)),), ((low, pl.ds(0, split)), (high, pl.ds(0, h))),
+    )
+
+    def late_in(rows):
+        return pltpu.make_async_remote_copy(
+            src_ref=deltas.at[1, d, rows, tail], dst_ref=late.at[d, rows],
+            send_sem=l_sem.at[0], recv_sem=l_sem.at[1],
+            device_id=(partner, d), device_id_type=MESH,
+        )
+
+    def late_hop(way, k):
+        owner = owner_of(way, k)
+        return pltpu.make_async_remote_copy(
+            src_ref=late.at[owner], dst_ref=late.at[owner],
+            send_sem=lh_send.at[way, k], recv_sem=lh_recv.at[way, k],
+            device_id=(s, ahead(way)), device_id_type=MESH,
+        )
+
+    def late_out(way, k):
+        owner = owner_of(way, k)
+        return pltpu.make_async_remote_copy(
+            src_ref=late.at[owner], dst_ref=deltas.at[1, owner, pl.ds(0, tokens), tail],
+            send_sem=lo_send.at[way, k], recv_sem=lo_recv.at[way, k],
+            device_id=(partner, d), device_id_type=MESH,
+        )
+
+    def delta_hop(a, way, k, rows, cols):
         owner = d - k if way == 0 else d + k
         return pltpu.make_async_remote_copy(
-            src_ref=deltas.at[a, owner, rows], dst_ref=deltas.at[a, owner, rows],
+            src_ref=deltas.at[a, owner, rows, cols], dst_ref=deltas.at[a, owner, rows, cols],
             send_sem=d_send.at[a, way, k], recv_sem=d_recv.at[a, way, k],
             device_id=(s, d + 1 if way == 0 else d - 1), device_id_type=MESH,
         )
@@ -243,9 +272,14 @@
     def share_delta(a, rows, delta):
         deltas[a, d, rows] = delta
         for way in range(2):
-            @pl.when(reach(way, 0))
+            for side, cols in delta_variants[a]:
+                @pl.when(both(side, reach(way, 0)))
+                def _():
+                    delta_hop(a, way, 0, rows, cols).start()
+        if a == 1:
+            @pl.when(low)
             def _():
-                delta_hop(a, way, 0, rows).start()
+                late_in(rows).start()
 
     first, second = pl.ds(0, h), pl.ds(h, h)
 
@@ -314,22 +348,64 @@
         norms[a, d] = norms_own[a, d]
     others, whole = pl.ds(0, n - 1), pl.ds(0, tokens)
     for k in range(1, n):
-        for a, out in ((1, g_out), (0, f_out)):
+        for a in (1, 0):
+            for way in range(2):
+                for side, cols in delta_variants[a]:
+                    @pl.when(both(side, arrives(way, k)))
+                    def _():
+                        wait_bytes(
+                            deltas.at[a, owner_of(way, k), whole, cols], d_recv.at[a, way, k - 1]
+                        )
+
+                    if k < n - 1:
+                        @pl.when(both(side, reach(way, k)))
+                        def _():
+                            delta_hop(a, way, k, whole, cols).start()
+    for a, out in ((0, f_out), (1, g_out)):
+        if a == 1:
+            for k in range(1, n):
+                for way in range(2):
+                    @pl.when(both(low, arrives(way, k)))
+                    def _():
+                        wait_bytes(deltas.at[1, owner_of(way, k), whole, tail], lo_recv.at[way, k])
+        wait_bytes(norms.at[a, others], n_recv.at[a])
+        out[...] = lax.dot_general(
+            norms[a].reshape(n * tokens, part), deltas[a].reshape(n * tokens, h),
+            (((0,), (0,)), ((), ())), preferred_element_type=f32,
+        )
+
+    @pl.when(high)
+    def _():
+        wait_bytes(late.at[d], l_sem.at[1])
+        for way in range(2):
+            @pl.when(reach(way, 0))
+            def _():
+                late_hop(way, 0).start()
+        for k in range(1, n):
             for way in range(2):
                 @pl.when(arrives(way, k))
                 def _():
-                    wait_bytes(deltas.at[a, d - k if way == 0 else d + k], d_recv.at[a, way, k - 1])
-
+                    wait_bytes(late.at[owner_of(way, k)], lh_recv.at[way, k - 1])
+                    if k < n - 1:
+                        @pl.when(reach(way, k))
+                        def _():
+                            late_hop(way, k).start()
+                    late_out(way, k).start()
+        for k in range(n):
+            for way in range(2):
                 if k < n - 1:
                     @pl.when(reach(way, k))
                     def _():
-                        delta_hop(a, way, k, whole).start()
-            if k == n - 1:
-                wait_bytes(norms.at[a, others], n_recv.at[a])
-                out[...] = lax.dot_general(
-                    norms[a].reshape(n * tokens, part), deltas[a].reshape(n * tokens, h),
-                    (((0,), (0,)), ((), ())), preferred_element_type=f32,
-                )
+                        late_hop(way, k).wait_send()
+                if k > 0:
+                    @pl.when(arrives(way, k))
+                    def _():
+                        late_out(way, k).wait_send()
+
+    @pl.when(low)
+    def _():
+        wait_bytes(late.at[d], l_sem.at[0])
+
     wait_bytes(gain_parts.at[others], c_recv)
     total = gain_parts[0]
     for e in range(1, n):
@@ -340,9 +416,12 @@
         wait_bytes(norms.at[a, others], n_send.at[a])
         for k in range(n - 1):
             for way in range(2):
-                @pl.when(reach(way, k))
-                def _():
-                    wait_bytes(deltas.at[a, d - k if way == 0 else d + k], d_send.at[a, way, k])
+                for side, cols in delta_variants[a]:
+                    @pl.when(both(side, reach(way, k)))
+                    def _():
+                        wait_bytes(
+                            deltas.at[a, owner_of(way, k), whole, cols], d_send.at[a, way, k]
+                        )
     wait_bytes(gain_parts.at[others], c_send)
 
     @pl.when(has_below)
@@ -398,6 +477,7 @@
             pltpu.VMEM((h, h), bf16),
             pltpu.VMEM((h, h), bf16),
             pltpu.VMEM((2, n, part, h // 8), bf16),
+            pltpu.VMEM((n, tokens, h // 2), bf16),
             pltpu.VMEM((4, tokens, h), bf16),
             pltpu.VMEM((4, tokens, h), bf16),
             pltpu.VMEM((4, tokens // blocks, h), f32),
@@ -406,6 +486,11 @@
             pltpu.VMEM((2, n, tokens, part), bf16),
             pltpu.VMEM((2, n, tokens, h), bf16),
             pltpu.VMEM((n, 2, h), f32),
+            dma((2,)),
+            dma((2, n)),
+            dma((2, n)),
+            dma((2, n)),
+            dma((2, n)),
             dma((2,)),
             dma((2,)),
             dma((2,)),

time: 152 us -> 149 us (0.980)
  Pallas kernels: 145 us -> 141 us
    pallas_call x1, Pallas kernels: 145 us -> 141 us  [shards(): pl.pallas_call(functools.partial(kernel, n, sections, blocks), out_shape=...]
where the time goes in v4:
time: 149 us
  Pallas kernels  141 us (95%)
  local copies, waits for them, and re-layouts  6.39 us (4%)
    pallas_call x1, Pallas kernels, shards(): pl.pallas_call(functools.partial(kernel, n, sections, blocks), out_shape=...  141 us
    unnamed x13, local copies, waits for them, and re-layouts  6.39 us

profile of v4, /device:TPU:0, one launch (start us, length us, event | category | flops | bytes accessed | tf_op | source)
XLA Modules:
  0.0 148.5 jit_solution(13580117086515551666)
XLA Ops:
  0.6 141.5 %shard_map.92 = (f32[128,2048]{1,0:T(8,128)}, bf16[128,2048]{1,0:T(8,128)(2,1)}, f32[256,1024]{1,0:T(8,128)}, f32[256,1024]{1,0:T(8,128)}, f32[2,1024]{1,0:T(2,128)}) custom-call(f32[128,2048]{1,0:T(8,128)} %pair_ref.1, bf16[128,2048]{1,0:T(8,128)(2,1)} %grad_ref.1, bf16[256,1024]{1,0:T(8,128)(2,1)} %bitcast.11, bf16[256,1024]{1,0:T(8,128)(2,1)} %bitcast.12, ...), custom_call_target="tpu_custom_call" | custom-call | tf_op jit(solution)/shard_map/pallas_call | solution.py:463
  142.1 0.0 copy-start.2
  142.1 0.0 copy-start.1
  142.1 2.4 %copy.15 = f32[1,128,2048]{2,1,0:T(8,128)} copy(f32[1,128,2048]{2,1,0:T(8,128)} %bitcast.10) | data formatting | bytes 2097152
  144.5 0.0 copy-done.2
  144.5 0.8 copy.16
  145.3 0.0 copy-done.1
  145.3 0.0 copy-start
  145.3 1.0 copy.17
  146.3 0.6 copy-done
  146.9 0.0 copy-start.3
  146.9 1.0 copy.18
  147.9 0.0 copy-done.3
  147.9 0.6 copy.19
Async XLA Ops:
  142.1 2.4 %copy-start.2 = (bf16[128,2048]{1,0:T(8,128)(2,1)S(1)}, bf16[128,2048]{1,0:T(8,128)(2,1)}, u32[]{:S(2)}) copy-start(bf16[128,2048]{1,0:T(8,128)(2,1)} %get-tuple-element.11) | copy-start | bytes 1572868
  142.1 3.2 %copy-start.1 = (f32[256,1024]{1,0:T(8,128)S(1)}, f32[256,1024]{1,0:T(8,128)}, u32[]{:S(2)}) copy-start(f32[256,1024]{1,0:T(8,128)} %get-tuple-element.12) | copy-start | bytes 3145732
  145.3 1.6 %copy-start = (f32[256,1024]{1,0:T(8,128)S(1)}, f32[256,1024]{1,0:T(8,128)}, u32[]{:S(2)}) copy-start(f32[256,1024]{1,0:T(8,128)} %get-tuple-element.13) | copy-start | bytes 3145732
  146.9 1.0 copy-start.3

commit v5 on v4

--- a/solution.py
+++ b/solution.py
@@ -361,6 +361,14 @@
                         @pl.when(both(side, reach(way, k)))
                         def _():
                             delta_hop(a, way, k, whole, cols).start()
+    @pl.when(high)
+    def _():
+        wait_bytes(late.at[d], l_sem.at[1])
+        for way in range(2):
+            @pl.when(reach(way, 0))
+            def _():
+                late_hop(way, 0).start()
+
     for a, out in ((0, f_out), (1, g_out)):
         if a == 1:
             for k in range(1, n):
@@ -376,11 +384,6 @@
 
     @pl.when(high)
     def _():
-        wait_bytes(late.at[d], l_sem.at[1])
-        for way in range(2):
-            @pl.when(reach(way, 0))
-            def _():
-                late_hop(way, 0).start()
         for k in range(1, n):
             for way in range(2):
                 @pl.when(arrives(way, k))

time: 149 us -> 148 us (level)
  no operation moved by 1% of the time
where the time goes in v5:
time: 148 us
  Pallas kernels  141 us (95%)
  local copies, waits for them, and re-layouts  6.39 us (4%)
    pallas_call x1, Pallas kernels, shards(): pl.pallas_call(functools.partial(kernel, n, sections, blocks), out_shape=...  141 us
    unnamed x13, local copies, waits for them, and re-layouts  6.39 us

profile of v5, /device:TPU:0, one launch (start us, length us, event | category | flops | bytes accessed | tf_op | source)
XLA Modules:
  0.0 147.6 jit_solution(2579741044289205113)
XLA Ops:
  0.6 140.5 %shard_map.92 = (f32[128,2048]{1,0:T(8,128)}, bf16[128,2048]{1,0:T(8,128)(2,1)}, f32[256,1024]{1,0:T(8,128)}, f32[256,1024]{1,0:T(8,128)}, f32[2,1024]{1,0:T(2,128)}) custom-call(f32[128,2048]{1,0:T(8,128)} %pair_ref.1, bf16[128,2048]{1,0:T(8,128)(2,1)} %grad_ref.1, bf16[256,1024]{1,0:T(8,128)(2,1)} %bitcast.11, bf16[256,1024]{1,0:T(8,128)(2,1)} %bitcast.12, ...), custom_call_target="tpu_custom_call" | custom-call | tf_op jit(solution)/shard_map/pallas_call | solution.py:466
  141.2 0.0 copy-start.2
  141.2 0.0 copy-start.1
  141.2 2.4 %copy.15 = f32[1,128,2048]{2,1,0:T(8,128)} copy(f32[1,128,2048]{2,1,0:T(8,128)} %bitcast.10) | data formatting | bytes 2097152
  143.6 0.0 copy-done.2
  143.6 0.8 copy.16
  144.4 0.0 copy-done.1
  144.4 0.0 copy-start
  144.4 1.0 copy.17
  145.4 0.6 copy-done
  146.0 0.0 copy-start.3
  146.0 1.0 copy.18
  147.0 0.0 copy-done.3
  147.0 0.6 copy.19
Async XLA Ops:
  141.2 2.4 %copy-start.2 = (bf16[128,2048]{1,0:T(8,128)(2,1)S(1)}, bf16[128,2048]{1,0:T(8,128)(2,1)}, u32[]{:S(2)}) copy-start(bf16[128,2048]{1,0:T(8,128)(2,1)} %get-tuple-element.11) | copy-start | bytes 1572868
  141.2 3.2 %copy-start.1 = (f32[256,1024]{1,0:T(8,128)S(1)}, f32[256,1024]{1,0:T(8,128)}, u32[]{:S(2)}) copy-start(f32[256,1024]{1,0:T(8,128)} %get-tuple-element.12) | copy-start | bytes 3145732
  144.4 1.6 %copy-start = (f32[256,1024]{1,0:T(8,128)S(1)}, f32[256,1024]{1,0:T(8,128)}, u32[]{:S(2)}) copy-start(f32[256,1024]{1,0:T(8,128)} %get-tuple-element.13) | copy-start | bytes 3145732
  146.0 1.0 copy-start.3
